TPU v7x, 32 devices: a whole 2x2x4 slice. The times are simulated.
32 devices in a mesh: dp: 8 (over z, y), mp: 4 (over x, core).
Axes of the slice: x: 2, y: 2, z: 4, core: 2. Of those that a mesh axis runs over, the one named last changes fastest.
Arguments:
- gradient: bfloat16 [8, 64, 14336], P('dp', None, 'mp'), may hold values from -6 to 6
- momentum: float32 [8, 64, 14336], P('dp', None, 'mp'), may hold values from -6 to 6
- weights: float32 [64, 14336], P(None, 'mp'), may hold values from -6 to 6
- positions: int32 [8, 1, 224, 32], P('dp', None, 'mp'), may hold values from 0 to 4095, as said below
Outputs:
- new_momentum: float32 [8, 64, 14336], P('dp', None, 'mp')
- new_weights: float32 [64, 14336], P(None, 'mp')
Inputs may be any that keep to these rules, and one draw needn't show every extreme that they name: Within one span of one replica the 32 positions are all different.
All inputs are finite; a program needn't handle non-finite values.
Results may differ from a plain program's by a relative error of at most 0.0003.
Values sent between devices are 32-bit elements; how exact they have to be, the bound alone decides.
A program may use at most 64 MiB of HBM per device.

v0:
```python
import functools

import jax
import jax.numpy as jnp
import numpy as np
from jax import lax
from jax.experimental import pallas as pl
from jax.experimental.pallas import tpu as pltpu
from jax.sharding import PartitionSpec as P

QUAD = 256
PAIR = 128
GROUP = 8
F32 = jnp.float32
BF16 = jnp.bfloat16


def dct_table():
    column = np.arange(64, dtype=np.float64)
    freq = column[:, None]
    factor = np.where(freq == 0, np.sqrt(1.0 / 64), np.sqrt(2.0 / 64))
    return factor * np.cos(np.pi * (2.0 * column[None, :] + 1.0) * freq / 128.0)


def halves(table):
    high = np.asarray(table, np.float32).astype(jnp.bfloat16)
    low = np.asarray(table - high.astype(np.float64), np.float32).astype(jnp.bfloat16)
    return high, low


def side_tables():
    table = dct_table()
    rows, columns = [], []
    for row, column in ((table, table.T), (table.T, table)):
        high, low = halves(row)
        rows.append(np.concatenate([high, low, high, low], axis=1))
        columns.append(np.concatenate(halves(np.kron(np.eye(2), column)), axis=1))
    return np.stack(rows), np.stack(columns)


def split(value):
    high = value.astype(BF16)
    return high, (value - high.astype(F32)).astype(BF16)


def dot(a, b):
    return jnp.dot(a, b, preferred_element_type=F32)


def dot_t(a, b):
    return lax.dot_general(a, b, (((1,), (1,)), ((), ())), preferred_element_type=F32)


def row_transform(table, value):
    high, low = split(value)
    return dot(table, jnp.concatenate([high, high, low, low], axis=0))


def column_transform(both, table):
    result = dot(both, jnp.concatenate([table, table], axis=0))
    return result[:, :PAIR] + result[:, PAIR:]


def counting(rows, lanes):
    count = lax.broadcasted_iota(jnp.int32, (rows, lanes), 0).astype(F32)
    return count.astype(BF16).reshape(-1, 16, lanes)


def spread(row):
    return jnp.broadcast_to(row, (16, row.shape[1])).astype(BF16)[None]


def flat(tiles):
    return tiles.reshape(-1, tiles.shape[-1])


def frequencies(places):
    return (places // 64).astype(F32), (places % 64).astype(F32)


def lane_part(shape):
    return lax.broadcasted_iota(jnp.int32, shape, 1) // 32


def regroup(members, part):
    result = []
    for start in range(0, GROUP, 4):
        joined = None
        for place in range(4):
            member = members[start + place]
            shift = (place - part) % 4 * 32
            moved = pltpu.roll(member, shift, axis=1) if shift else member
            joined = moved if joined is None else jnp.where(lane_part(moved.shape) == place, moved, joined)
        result.append(joined)
    return jnp.concatenate(result, axis=1)


def loop(count, body):
    if count <= 16:
        for step in range(count):
            body(step)
    else:
        lax.fori_loop(0, count, lambda step, carry: (body(step), carry)[1], 0)


def kernel(
    replicas, parts, entries,
    gradient_ref, momentum_ref, weights_ref, places_hbm, rows_hbm, columns_hbm,
    summed, update,
    grad, mom, wts, places_ref, rows_ref, columns_ref, flipped, both, coefs,
    place_lists, value_lists, row_parts, column_parts, value_parts, squares,
    in_sem, place_send, place_recv, value_send, value_recv, square_send, square_recv,
):
    me, mine = lax.axis_index("dp"), lax.axis_index("mp")
    width = summed.shape[1]
    quads = width // QUAD

    loads = [
        pltpu.make_async_copy(source, target, in_sem.at[index])
        for index, (source, target) in enumerate(
            (
                (places_hbm.at[0, 0], places_ref), (rows_hbm, rows_ref), (gradient_ref.at[0], grad),
                (momentum_ref.at[0], mom), (columns_hbm, columns_ref), (weights_ref, wts),
            )
        )
    ]
    barrier = pltpu.get_barrier_semaphore()

    def greet_replica(step):
        pl.semaphore_signal(
            barrier, inc=1, device_id={"dp": lax.rem(me + step + 1, replicas)},
            device_id_type=pl.DeviceIdType.MESH,
        )

    def greet_part(step):
        pl.semaphore_signal(
            barrier, inc=1, device_id={"mp": lax.rem(mine + step + 1, parts)},
            device_id_type=pl.DeviceIdType.MESH,
        )

    loop(replicas - 1, greet_replica)
    loop(parts - 1, greet_part)
    for load in loads:
        load.start()

    def block(index):
        return pl.ds(index * QUAD, QUAD)

    def rows(index):
        return pl.ds(index * 64, 64)

    def quad(ref, index):
        return jnp.concatenate([ref[rows(2 * index), :], ref[rows(2 * index + 1), :]], axis=1)

    def keep(index, value):
        for half, part in enumerate(split(value)):
            for side in range(2):
                both[rows(2 * index + side), half * PAIR : (half + 1) * PAIR] = part[
                    :, side * PAIR : (side + 1) * PAIR
                ]

    def keep_pair(index, value):
        for half, part in enumerate(split(value)):
            both[rows(index), half * PAIR : (half + 1) * PAIR] = part

    def list_copy(lists, send_sem, recv_sem, step, slot):
        return pltpu.make_async_remote_copy(
            src_ref=lists.at[slot], dst_ref=lists.at[slot],
            send_sem=send_sem.at[step], recv_sem=recv_sem.at[slot],
            device_id={"dp": lax.rem(me + step + 1, replicas)},
            device_id_type=pl.DeviceIdType.MESH,
        )

    def place_copy(step, slot):
        return list_copy(place_lists, place_send, place_recv, step, slot)

    def value_copy(step, slot):
        return list_copy(value_lists, value_send, value_recv, step, slot)

    groups = place_lists.shape[0] // GROUP
    for slot in range(replicas, groups * GROUP):
        place_lists[slot, :, :] = jnp.zeros(place_lists.shape[1:], F32)
        value_lists[slot, :, :] = jnp.zeros(value_lists.shape[1:], F32)

    loads[0].wait()
    flipped[...] = jnp.transpose(places_ref[...])
    places = jnp.concatenate(
        [flipped[pl.ds(part, quads, stride=4), :] for part in range(4)], axis=1
    )
    place_lists[me, 0:quads, :] = places.astype(F32)

    for load in loads[1:4]:
        load.wait()
    for index in range(quads):
        value = 0.9 * mom[:, block(index)] + grad[:, block(index)].astype(F32)
        summed[:, block(index)] = value
        keep(index, row_transform(rows_ref[0], value))

    pl.semaphore_wait(barrier, replicas - 1 + parts - 1)
    loop(replicas - 1, lambda step: place_copy(step, me).start())

    loads[4].wait()
    coefs[...] = column_transform(both[...], columns_ref[0])

    zero, one = jnp.zeros((), BF16), jnp.ones((), BF16)
    count_quad = counting(QUAD, PAIR)
    row_freqs, spots = frequencies(places)
    spots = spots + (lane_part(places.shape) * 64).astype(F32)
    for index in range(quads):
        row_hot = flat(jnp.where(count_quad[:4] == spread(row_freqs[index : index + 1, :]), one, zero))
        column_hot = flat(jnp.where(count_quad == spread(spots[index : index + 1, :]), one, zero))
        value = quad(coefs, index)
        found = dot(jnp.concatenate(split(value), axis=0), column_hot)
        found = (found[:64, :] + found[64:, :]) * row_hot.astype(F32)
        value_lists[me, index : index + 1, :] = jnp.sum(found, axis=0, keepdims=True)
        keep(index, value * dot_t(row_hot, column_hot))

    loop(replicas - 1, lambda step: value_copy(step, me).start())

    coefs[...] = column_transform(both[...], columns_ref[1])
    for index in range(quads):
        back = row_transform(rows_ref[1], quad(coefs, index))
        summed[:, block(index)] = summed[:, block(index)] - back

    def source(step):
        return lax.rem(me + replicas - step - 1, replicas)

    def regroup_places(group):
        members = [
            frequencies(place_lists[group * GROUP + member, :, :].astype(jnp.int32))
            for member in range(GROUP)
        ]
        for part in range(4):
            row_parts[group, part, :, :] = regroup([member[0] for member in members], part)
            column_parts[group, part, :, :] = regroup([member[1] for member in members], part)

    def regroup_values(group):
        members = [value_lists[group * GROUP + member, :, :] for member in range(GROUP)]
        for part in range(4):
            value_parts[group, part, :, :] = regroup(members, part)

    loop(replicas - 1, lambda step: place_copy(step, source(step)).wait_recv())
    loop(groups, regroup_places)
    loop(replicas - 1, lambda step: value_copy(step, source(step)).wait_recv())
    loop(groups, regroup_values)

    count_group = counting(64, GROUP * 32)

    def decode(group, index, part):
        line = slice(index, index + 1)
        row_hot = flat(jnp.where(count_group == spread(row_parts[group, part, line, :]), one, zero))
        here = count_group == spread(column_parts[group, part, line, :])
        high, low = split(jnp.broadcast_to(value_parts[group, part, line, :], (16, GROUP * 32)))
        right = jnp.concatenate(
            [flat(jnp.where(here, high[None], zero)), flat(jnp.where(here, low[None], zero))], axis=0
        )
        result = dot_t(row_hot, right)
        return result + pltpu.roll(result, 64, axis=1)

    def decode_pair(group, index, side):
        left, right = (decode(group, index, 2 * side + place) for place in range(2))
        return jnp.where(lane_part(left.shape) < 2, left, right)

    square = jnp.zeros((8, PAIR), F32)
    for index in range(quads):
        for side in range(2):
            total = decode_pair(0, index, side)
            if groups > 1:
                total = lax.fori_loop(
                    1, groups, lambda step, acc: acc + decode_pair(step, index, side), total
                )
            square = square + jnp.sum((total * total).reshape(8, 8, PAIR), axis=0)
            keep_pair(2 * index + side, total)

    squares[mine, :, :] = square

    def square_copy(step, slot):
        return pltpu.make_async_remote_copy(
            src_ref=squares.at[slot], dst_ref=squares.at[slot],
            send_sem=square_send.at[step], recv_sem=square_recv.at[slot],
            device_id={"mp": lax.rem(mine + step + 1, parts)},
            device_id_type=pl.DeviceIdType.MESH,
        )

    loop(parts - 1, lambda step: square_copy(step, mine).start())

    coefs[...] = column_transform(both[...], columns_ref[1])
    for index in range(quads):
        update[:, block(index)] = row_transform(rows_ref[1], quad(coefs, index))

    loop(
        parts - 1,
        lambda step: square_copy(step, lax.rem(mine + parts - step - 1, parts)).wait_recv(),
    )
    loads[5].wait()
    meansq = jnp.sum(jnp.sum(squares[...], axis=0)) / entries
    factor = lax.rsqrt(jnp.full((1, QUAD), meansq + 1.0, F32))
    for index in range(quads):
        update[:, block(index)] = wts[:, block(index)] - update[:, block(index)] * factor
    loop(replicas - 1, lambda step: place_copy(step, me).wait_send())
    loop(replicas - 1, lambda step: value_copy(step, me).wait_send())
    loop(parts - 1, lambda step: square_copy(step, mine).wait_send())


def deliver(summed, update, out_momentum_ref, out_weights_ref, out_sem):
    stores = (
        pltpu.make_async_copy(summed, out_momentum_ref.at[0], out_sem.at[0]),
        pltpu.make_async_copy(update, out_weights_ref, out_sem.at[1]),
    )
    for store in stores:
        store.start()
    for store in stores:
        store.wait()


def local(replicas, parts, gradient, momentum, weights, positions):
    height, width = weights.shape
    quads = width // QUAD
    row_tables, column_tables = side_tables()
    anywhere = pl.BlockSpec(memory_space=pl.ANY)
    vmem = pl.BlockSpec(memory_space=pltpu.VMEM)
    listed = -(-quads // 8) * 8
    groups = -(-replicas // GROUP)
    entries = positions.shape[-1]
    results = pl.pallas_call(
        functools.partial(kernel, replicas, parts, float(height * width * parts)),
        out_shape=(
            jax.ShapeDtypeStruct(weights.shape, F32),
            jax.ShapeDtypeStruct(weights.shape, F32),
        ),
        in_specs=[pl.BlockSpec(memory_space=pltpu.HBM)] * 6,
        out_specs=(vmem, vmem),
        scratch_shapes=[
            pltpu.VMEM((height, width), BF16),
            pltpu.VMEM((height, width), F32),
            pltpu.VMEM((height, width), F32),
            pltpu.VMEM((entries, 4 * quads), jnp.int32),
            pltpu.VMEM(row_tables.shape, BF16),
            pltpu.VMEM(column_tables.shape, BF16),
            pltpu.VMEM((4 * quads, entries), jnp.int32),
            pltpu.VMEM((2 * quads * 64, QUAD), BF16),
            pltpu.VMEM((2 * quads * 64, PAIR), F32),
            pltpu.VMEM((groups * GROUP, listed, PAIR), F32),
            pltpu.VMEM((groups * GROUP, listed, PAIR), F32),
            pltpu.VMEM((groups, 4, listed, GROUP * 32), F32),
            pltpu.VMEM((groups, 4, listed, GROUP * 32), F32),
            pltpu.VMEM((groups, 4, listed, GROUP * 32), F32),
            pltpu.VMEM((parts, 8, PAIR), F32),
            pltpu.SemaphoreType.DMA((6,)),
            pltpu.SemaphoreType.DMA((replicas,)),
            pltpu.SemaphoreType.DMA((replicas,)),
            pltpu.SemaphoreType.DMA((replicas,)),
            pltpu.SemaphoreType.DMA((replicas,)),
            pltpu.SemaphoreType.DMA((parts,)),
            pltpu.SemaphoreType.DMA((parts,)),
        ],
        compiler_params=pltpu.CompilerParams(
            collective_id=0, has_side_effects=True, vmem_limit_bytes=24 * 1024 * 1024
        ),
    )(
        *(
            pltpu.with_memory_space_constraint(array, pltpu.HBM)
            for array in (
                gradient, momentum, weights, jnp.swapaxes(positions, 2, 3),
                jnp.asarray(row_tables), jnp.asarray(column_tables),
            )
        )
    )
    return pl.pallas_call(
        deliver,
        out_shape=(
            jax.ShapeDtypeStruct(momentum.shape, F32),
            jax.ShapeDtypeStruct(weights.shape, F32),
        ),
        in_specs=[vmem] * 2,
        out_specs=(anywhere, anywhere),
        scratch_shapes=[pltpu.SemaphoreType.DMA((2,))],
        compiler_params=pltpu.CompilerParams(vmem_limit_bytes=8 * 1024 * 1024),
    )(*results)


def solution(mesh):
    placed = (P("dp", None, "mp"), P("dp", None, "mp"), P(None, "mp"), P("dp", None, "mp", None))
    return jax.shard_map(
        functools.partial(local, mesh.shape["dp"], mesh.shape["mp"]),
        mesh=mesh,
        in_specs=placed,
        out_specs=(P("dp", None, "mp"), P(None, "mp")),
        check_vma=False,
    )
```

profile of v0, /device:TPU:0, one launch (start us, length us, event | category | flops | bytes accessed | tf_op | source)
XLA Modules:
  0.0 17.8 jit_solution(11253053146600104421)
XLA Ops:
  0.6 15.9 %shard_map.77 = (f32[64,3584]{1,0:T(8,128)S(1)}, f32[64,3584]{1,0:T(8,128)S(1)}) custom-call(bf16[1,64,3584]{2,1,0:T(8,128)(2,1)} %gradient_ref.1, f32[1,64,3584]{2,1,0:T(8,128)} %momentum_ref.1, f32[64,3584]{1,0:T(8,128)} %weights_ref.1, s32[1,1,32,56]{3,2,1,0:T(8,128)} %bitcast.1, bf16[2,64,256]{2,1,0:T(8,128)(2,1)} %constant.4.clone.rows_hbm, ...), custom_call_target="tpu_custom_call" | custom-call | tf_op jit(solution)/shard_map/pallas_call | solution.py:325
  16.6 1.2 %shard_map.78 = (f32[1,64,3584]{2,1,0:T(8,128)}, f32[64,3584]{1,0:T(8,128)}) custom-call(f32[64,3584]{1,0:T(8,128)S(1)} %get-tuple-element.4.summed, f32[64,3584]{1,0:T(8,128)S(1)} %get-tuple-element.5.update), custom_call_target="tpu_custom_call" | custom-call | tf_op jit(solution)/shard_map/pallas_call | solution.py:369
where the time goes:
time: 18 us; the launch traced here: 17.8 us
  Pallas kernels  17.2 us (96%)
  between operations  0.64 us (4%)
    pallas_call x1, Pallas kernels, local(): pl.pallas_call(functools.partial(kernel, replicas, parts, float(height *...  15.9 us
    pallas_call x1, Pallas kernels, local(): pl.pallas_call(deliver, out_shape=(jax.ShapeDtypeStruct(momentum.shape, F...  1.24 us

commit v1 on v0

v1 whole, which is shorter than its diff:
```python
import functools

import jax
import jax.numpy as jnp
import numpy as np
from jax import lax
from jax.experimental import pallas as pl
from jax.experimental.pallas import tpu as pltpu
from jax.sharding import PartitionSpec as P

QUAD = 256
PAIR = 128
GROUP = 8
CHUNKS = 2
F32 = jnp.float32
BF16 = jnp.bfloat16


def dct_table():
    column = np.arange(64, dtype=np.float64)
    freq = column[:, None]
    factor = np.where(freq == 0, np.sqrt(1.0 / 64), np.sqrt(2.0 / 64))
    return factor * np.cos(np.pi * (2.0 * column[None, :] + 1.0) * freq / 128.0)


def halves(table):
    high = np.asarray(table, np.float32).astype(jnp.bfloat16)
    low = np.asarray(table - high.astype(np.float64), np.float32).astype(jnp.bfloat16)
    return high, low


def side_tables():
    table = dct_table()
    high, low = halves(table.T)
    gather = np.concatenate([high, low], axis=0)
    rows = np.concatenate([high, low, high, low], axis=1)
    columns = np.concatenate(halves(np.kron(np.eye(2), table)), axis=1)
    return gather, rows, columns


def split(value):
    high = value.astype(BF16)
    return high, (value - high.astype(F32)).astype(BF16)


def dot(a, b):
    return jnp.dot(a, b, preferred_element_type=F32)


def dot_t(a, b):
    return lax.dot_general(a, b, (((1,), (1,)), ((), ())), preferred_element_type=F32)


def row_transform(table, value):
    high, low = split(value)
    return dot(table, jnp.concatenate([high, high, low, low], axis=0))


def column_transform(both, table):
    result = dot(both, jnp.concatenate([table, table], axis=0))
    return result[:, :PAIR] + result[:, PAIR:]


def counting(rows, lanes):
    count = lax.broadcasted_iota(jnp.int32, (rows, lanes), 0).astype(F32)
    return count.astype(BF16).reshape(-1, 16, lanes)


def spread(row):
    return jnp.broadcast_to(row, (16, row.shape[1])).astype(BF16)[None]


def flat(tiles):
    return tiles.reshape(-1, tiles.shape[-1])


def frequencies(places):
    return (places // 64).astype(F32), (places % 64).astype(F32)


def lane_part(shape):
    return lax.broadcasted_iota(jnp.int32, shape, 1) // 32


def regroup(members, part):
    result = []
    for start in range(0, GROUP, 4):
        joined = None
        for place in range(4):
            member = members[start + place]
            shift = (place - part) % 4 * 32
            moved = pltpu.roll(member, shift, axis=1) if shift else member
            joined = moved if joined is None else jnp.where(lane_part(moved.shape) == place, moved, joined)
        result.append(joined)
    return jnp.concatenate(result, axis=1)


def loop(count, body):
    if count <= 16:
        for step in range(count):
            body(step)
    else:
        lax.fori_loop(0, count, lambda step, carry: (body(step), carry)[1], 0)


def kernel(
    replicas, parts, chunks,
    gradient_ref, momentum_ref, weights_ref, places_hbm, gather_hbm, rows_hbm, columns_hbm,
    summed, update, wts, squares,
    grad, mom, places_ref, gather_ref, rows_ref, columns_ref, flipped, row_side, column_side, both, coefs,
    place_lists, value_lists, row_parts, column_parts, value_parts,
    in_sem, chunk_sem, place_send, place_recv, value_send, value_recv, square_send, square_recv,
):
    me, mine = lax.axis_index("dp"), lax.axis_index("mp")
    width = summed.shape[1]
    quads = width // QUAD
    per = quads // chunks
    tall = place_lists.shape[1] // chunks

    def block(index):
        return pl.ds(index * QUAD, QUAD)

    def rows(index):
        return pl.ds(index * 64, 64)

    def line(index):
        return index // per * tall + index % per

    def chunk_loads(chunk):
        span = pl.ds(chunk * per * QUAD, per * QUAD)
        return [
            pltpu.make_async_copy(source.at[0, :, span], target.at[:, span], chunk_sem.at[chunk, index])
            for index, (source, target) in enumerate(((gradient_ref, grad), (momentum_ref, mom)))
        ]

    loads = [
        pltpu.make_async_copy(source, target, in_sem.at[index])
        for index, (source, target) in enumerate(
            (
                (places_hbm.at[0, 0], places_ref), (gather_hbm, gather_ref),
                (rows_hbm, rows_ref), (columns_hbm, columns_ref), (weights_ref, wts),
            )
        )
    ]
    for load in loads[:2]:
        load.start()
    for chunk in range(chunks):
        for load in chunk_loads(chunk):
            load.start()
    for load in loads[2:]:
        load.start()

    barrier = pltpu.get_barrier_semaphore()

    def greet_replica(step):
        pl.semaphore_signal(
            barrier, inc=1, device_id={"dp": lax.rem(me + step + 1, replicas)},
            device_id_type=pl.DeviceIdType.MESH,
        )

    def greet_part(step):
        pl.semaphore_signal(
            barrier, inc=1, device_id={"mp": lax.rem(mine + step + 1, parts)},
            device_id_type=pl.DeviceIdType.MESH,
        )

    loop(replicas - 1, greet_replica)
    loop(parts - 1, greet_part)

    def list_copy(lists, send_sem, recv_sem, step, slot, span):
        return pltpu.make_async_remote_copy(
            src_ref=lists.at[slot, span], dst_ref=lists.at[slot, span],
            send_sem=send_sem, recv_sem=recv_sem,
            device_id={"dp": lax.rem(me + step + 1, replicas)},
            device_id_type=pl.DeviceIdType.MESH,
        )

    def place_copy(step, slot):
        return list_copy(
            place_lists, place_send.at[step], place_recv.at[slot], step, slot, pl.ds(0, chunks * tall)
        )

    def value_copy(chunk, step, slot):
        return list_copy(
            value_lists, value_send.at[chunk, step], value_recv.at[chunk, slot],
            step, slot, pl.ds(chunk * tall, tall),
        )

    groups = place_lists.shape[0] // GROUP
    for slot in range(replicas, groups * GROUP):
        place_lists[slot, :, :] = jnp.zeros(place_lists.shape[1:], F32)
        value_lists[slot, :, :] = jnp.zeros(value_lists.shape[1:], F32)

    loads[0].wait()
    flipped[...] = jnp.transpose(places_ref[...])
    places = jnp.concatenate(
        [flipped[pl.ds(part, quads, stride=4), :] for part in range(4)], axis=1
    )
    for chunk in range(chunks):
        place_lists[me, chunk * tall : chunk * tall + per, :] = places[
            chunk * per : (chunk + 1) * per
        ].astype(F32)

    pl.semaphore_wait(barrier, replicas - 1 + parts - 1)
    loop(replicas - 1, lambda step: place_copy(step, me).start())

    zero, one = jnp.zeros((), BF16), jnp.ones((), BF16)
    count = counting(64, PAIR)
    row_freqs, column_freqs = frequencies(places)
    lanes = lane_part((64, PAIR))

    def hot(row):
        return flat(jnp.where(count == spread(row), one, zero))

    loads[1].wait()
    for index in range(quads):
        hots = [hot(freqs[index : index + 1, :]) for freqs in (row_freqs, column_freqs)]
        found = dot(gather_ref[...], jnp.concatenate(hots, axis=1))
        row_side[rows(index), :] = found[:64, :PAIR] + found[64:, :PAIR]
        for half in range(2):
            side = found[half * 64 : (half + 1) * 64, PAIR:]
            for part in range(4):
                column_side[pl.ds(index * QUAD + part * 64, 64), half * PAIR : (half + 1) * PAIR] = (
                    jnp.where(lanes == part, side, 0.0).astype(BF16)
                )

    for chunk in range(chunks):
        for load in chunk_loads(chunk):
            load.wait()
        for index in range(chunk * per, (chunk + 1) * per):
            value = 0.9 * mom[:, block(index)] + grad[:, block(index)].astype(F32)
            summed[:, block(index)] = value
            found = dot(jnp.concatenate(split(value), axis=0), column_side[block(index), :])
            found = found[:64, :] + found[64:, :]
            found = (found[:, :PAIR] + found[:, PAIR:]) * row_side[rows(index), :]
            value_lists[me, pl.ds(line(index), 1), :] = jnp.sum(found, axis=0, keepdims=True)
        loop(replicas - 1, lambda step: value_copy(chunk, step, me).start())

    for index in range(quads):
        scaled = row_side[rows(index), :] * value_lists[me, pl.ds(line(index), 1), :]
        high, low = split(scaled)
        left = jnp.concatenate(
            [jnp.concatenate([high, high], axis=1), jnp.concatenate([low, low], axis=1)], axis=0
        )
        back = dot_t(left, column_side[block(index), :])
        summed[:, block(index)] = summed[:, block(index)] - (back[:64, :] + back[64:, :])

    def source(step):
        return lax.rem(me + replicas - step - 1, replicas)

    def quad(ref, index):
        return jnp.concatenate([ref[rows(2 * index), :], ref[rows(2 * index + 1), :]], axis=1)

    def keep_pair(index, value):
        for half, part in enumerate(split(value)):
            both[rows(index), half * PAIR : (half + 1) * PAIR] = part

    def regroup_places(group):
        members = [
            frequencies(place_lists[group * GROUP + member, :, :].astype(jnp.int32))
            for member in range(GROUP)
        ]
        for part in range(4):
            row_parts[group, part, :, :] = regroup([member[0] for member in members], part)
            column_parts[group, part, :, :] = regroup([member[1] for member in members], part)

    def regroup_values(group, chunk):
        span = slice(chunk * tall, (chunk + 1) * tall)
        members = [value_lists[group * GROUP + member, span, :] for member in range(GROUP)]
        for part in range(4):
            value_parts[group, part, span, :] = regroup(members, part)

    loop(replicas - 1, lambda step: place_copy(step, source(step)).wait_recv())
    loop(groups, regroup_places)

    count_group = counting(64, GROUP * 32)

    def decode(group, index, part):
        place = slice(line(index), line(index) + 1)
        row_hot = flat(jnp.where(count_group == spread(row_parts[group, part, place, :]), one, zero))
        here = count_group == spread(column_parts[group, part, place, :])
        high, low = split(jnp.broadcast_to(value_parts[group, part, place, :], (16, GROUP * 32)))
        right = jnp.concatenate(
            [flat(jnp.where(here, high[None], zero)), flat(jnp.where(here, low[None], zero))], axis=0
        )
        result = dot_t(row_hot, right)
        return result + pltpu.roll(result, 64, axis=1)

    def decode_pair(group, index, side):
        left, right = (decode(group, index, 2 * side + place) for place in range(2))
        return jnp.where(lane_part(left.shape) < 2, left, right)

    square = jnp.zeros((8, PAIR), F32)
    for chunk in range(chunks):
        loop(replicas - 1, lambda step: value_copy(chunk, step, source(step)).wait_recv())
        loop(groups, lambda group: regroup_values(group, chunk))
        for index in range(chunk * per, (chunk + 1) * per):
            for side in range(2):
                total = decode_pair(0, index, side)
                if groups > 1:
                    total = lax.fori_loop(
                        1, groups, lambda step, acc: acc + decode_pair(step, index, side), total
                    )
                square = square + jnp.sum((total * total).reshape(8, 8, PAIR), axis=0)
                keep_pair(2 * index + side, total)

    squares[mine, :, :] = square

    def square_copy(step, slot):
        return pltpu.make_async_remote_copy(
            src_ref=squares.at[slot], dst_ref=squares.at[slot],
            send_sem=square_send.at[step], recv_sem=square_recv.at[slot],
            device_id={"mp": lax.rem(mine + step + 1, parts)},
            device_id_type=pl.DeviceIdType.MESH,
        )

    loop(parts - 1, lambda step: square_copy(step, mine).start())

    for load in loads[2:4]:
        load.wait()
    coefs[...] = column_transform(both[...], columns_ref[...])
    for index in range(quads):
        update[:, block(index)] = row_transform(rows_ref[...], quad(coefs, index))

    loads[4].wait()
    loop(replicas - 1, lambda step: place_copy(step, me).wait_send())
    for chunk in range(chunks):
        loop(replicas - 1, lambda step: value_copy(chunk, step, me).wait_send())
    loop(parts - 1, lambda step: square_copy(step, mine).wait_send())
    loop(
        parts - 1,
        lambda step: square_copy(step, lax.rem(mine + parts - step - 1, parts)).wait_recv(),
    )


def deliver(chunks, entries, summed, update, weights, squares, out_momentum_ref, out_weights_ref, result, out_sem):
    share = weights.shape[1] // chunks
    first = pltpu.make_async_copy(summed, out_momentum_ref.at[0], out_sem.at[chunks])
    first.start()
    meansq = jnp.sum(jnp.sum(squares[...], axis=0)) / entries
    factor = lax.rsqrt(jnp.full((1, share), meansq + 1.0, F32))
    stores = []
    for chunk in range(chunks):
        span = pl.ds(chunk * share, share)
        result[:, span] = weights[:, span] - update[:, span] * factor
        stores.append(pltpu.make_async_copy(result.at[:, span], out_weights_ref.at[:, span], out_sem.at[chunk]))
        stores[-1].start()
    first.wait()
    for store in stores:
        store.wait()


def local(replicas, parts, gradient, momentum, weights, positions):
    height, width = weights.shape
    quads = width // QUAD
    tables = side_tables()
    anywhere = pl.BlockSpec(memory_space=pl.ANY)
    vmem = pl.BlockSpec(memory_space=pltpu.VMEM)
    chunks = CHUNKS if quads % CHUNKS == 0 else 1
    listed = chunks * (-(-(quads // chunks) // 8) * 8)
    groups = -(-replicas // GROUP)
    entries = positions.shape[-1]
    wide = jax.ShapeDtypeStruct(weights.shape, F32)
    results = pl.pallas_call(
        functools.partial(kernel, replicas, parts, chunks),
        out_shape=(wide, wide, wide, jax.ShapeDtypeStruct((parts, 8, PAIR), F32)),
        in_specs=[pl.BlockSpec(memory_space=pltpu.HBM)] * 7,
        out_specs=(vmem,) * 4,
        scratch_shapes=[
            pltpu.VMEM((height, width), BF16),
            pltpu.VMEM((height, width), F32),
            pltpu.VMEM((entries, 4 * quads), jnp.int32),
            *[pltpu.VMEM(table.shape, BF16) for table in tables],
            pltpu.VMEM((4 * quads, entries), jnp.int32),
            pltpu.VMEM((quads * 64, PAIR), F32),
            pltpu.VMEM((quads * QUAD, QUAD), BF16),
            pltpu.VMEM((2 * quads * 64, QUAD), BF16),
            pltpu.VMEM((2 * quads * 64, PAIR), F32),
            pltpu.VMEM((groups * GROUP, listed, PAIR), F32),
            pltpu.VMEM((groups * GROUP, listed, PAIR), F32),
            pltpu.VMEM((groups, 4, listed, GROUP * 32), F32),
            pltpu.VMEM((groups, 4, listed, GROUP * 32), F32),
            pltpu.VMEM((groups, 4, listed, GROUP * 32), F32),
            pltpu.SemaphoreType.DMA((5,)),
            pltpu.SemaphoreType.DMA((chunks, 2)),
            pltpu.SemaphoreType.DMA((replicas,)),
            pltpu.SemaphoreType.DMA((replicas,)),
            pltpu.SemaphoreType.DMA((chunks, replicas)),
            pltpu.SemaphoreType.DMA((chunks, replicas)),
            pltpu.SemaphoreType.DMA((parts,)),
            pltpu.SemaphoreType.DMA((parts,)),
        ],
        compiler_params=pltpu.CompilerParams(
            collective_id=0, has_side_effects=True, vmem_limit_bytes=24 * 1024 * 1024
        ),
    )(
        *(
            pltpu.with_memory_space_constraint(array, pltpu.HBM)
            for array in (
                gradient, momentum, weights, jnp.swapaxes(positions, 2, 3), *map(jnp.asarray, tables),
            )
        )
    )
    return pl.pallas_call(
        functools.partial(deliver, chunks, float(height * width * parts)),
        out_shape=(
            jax.ShapeDtypeStruct(momentum.shape, F32),
            jax.ShapeDtypeStruct(weights.shape, F32),
        ),
        in_specs=[vmem] * 4,
        out_specs=(anywhere, anywhere),
        scratch_shapes=[pltpu.VMEM((height, width), F32), pltpu.SemaphoreType.DMA((chunks + 1,))],
        compiler_params=pltpu.CompilerParams(vmem_limit_bytes=8 * 1024 * 1024),
    )(*results)


def solution(mesh):
    placed = (P("dp", None, "mp"), P("dp", None, "mp"), P(None, "mp"), P("dp", None, "mp", None))
    return jax.shard_map(
        functools.partial(local, mesh.shape["dp"], mesh.shape["mp"]),
        mesh=mesh,
        in_specs=placed,
        out_specs=(P("dp", None, "mp"), P(None, "mp")),
        check_vma=False,
    )
```

time: 18 us -> 17.3 us (0.961)
  Pallas kernels: 17.2 us -> 16.4 us
    pallas_call x2, Pallas kernels: 17.2 us -> 16.4 us  [the longest x1 15.1 us: local(): pl.pallas_call(functools.partial(kernel, replicas, parts, chunks), out_sh...]
where the time goes in v1:
time: 17.3 us; the launch traced here: 17 us
  Pallas kernels  16.4 us (95%)
  between operations  0.64 us (4%)
    pallas_call x1, Pallas kernels, local(): pl.pallas_call(functools.partial(kernel, replicas, parts, chunks), out_sh...  15.1 us
    pallas_call x1, Pallas kernels, local(): pl.pallas_call(functools.partial(deliver, chunks, float(height * width *...  1.25 us

profile of v1, /device:TPU:0, one launch (start us, length us, event | category | flops | bytes accessed | tf_op | source)
XLA Modules:
  0.0 17.0 jit_solution(13895096446480319005)
XLA Ops:
  0.6 15.1 %shard_map.86 = (f32[64,3584]{1,0:T(8,128)S(1)}, f32[64,3584]{1,0:T(8,128)S(1)}, f32[64,3584]{1,0:T(8,128)S(1)}, f32[4,8,128]{2,1,0:T(8,128)S(1)}) custom-call(bf16[1,64,3584]{2,1,0:T(8,128)(2,1)} %gradient_ref.1, f32[1,64,3584]{2,1,0:T(8,128)} %momentum_ref.1, f32[64,3584]{1,0:T(8,128)} %weights_ref.1, s32[1,1,32,56]{3,2,1,0:T(8,128)} %bitcast.1, ...), custom_call_target="tpu_custom_call" | custom-call | tf_op jit(solution)/shard_map/pallas_call | solution.py:364
  15.8 1.2 %shard_map.87 = (f32[1,64,3584]{2,1,0:T(8,128)}, f32[64,3584]{1,0:T(8,128)}) custom-call(f32[64,3584]{1,0:T(8,128)S(1)} %get-tuple-element.6.summed, f32[64,3584]{1,0:T(8,128)S(1)} %get-tuple-element.7.update, f32[64,3584]{1,0:T(8,128)S(1)} %get-tuple-element.8.weights, f32[4,8,128]{2,1,0:T(8,128)S(1)} %get-tuple-element.9.squares), custom_call_target="tpu_custom_call" | custom-call | tf_op jit(solution)/shard_map/pallas_call | solution.py:404

commit v2 on v1

--- a/solution.py
+++ b/solution.py
@@ -11,9 +11,10 @@
 QUAD = 256
 PAIR = 128
 GROUP = 8
-CHUNKS = 2
+CHUNKS = 1
 F32 = jnp.float32
 BF16 = jnp.bfloat16
+F8 = jnp.float8_e4m3fn
 
 
 def dct_table():
@@ -103,12 +104,19 @@
         lax.fori_loop(0, count, lambda step, carry: (body(step), carry)[1], 0)
 
 
+def each(count, body):
+    if count == 1:
+        body(0)
+    else:
+        lax.fori_loop(0, count, lambda step, carry: (body(step), carry)[1], 0)
+
+
 def kernel(
     replicas, parts, chunks,
     gradient_ref, momentum_ref, weights_ref, places_hbm, gather_hbm, rows_hbm, columns_hbm,
     summed, update, wts, squares,
     grad, mom, places_ref, gather_ref, rows_ref, columns_ref, flipped, row_side, column_side, both, coefs,
-    place_lists, value_lists, row_parts, column_parts, value_parts,
+    place_lists, value_lists, low_parts, cell_parts, value_parts, hots, sums,
     in_sem, chunk_sem, place_send, place_recv, value_send, value_recv, square_send, square_recv,
 ):
     me, mine = lax.axis_index("dp"), lax.axis_index("mp")
@@ -201,9 +209,6 @@
             chunk * per : (chunk + 1) * per
         ].astype(F32)
 
-    pl.semaphore_wait(barrier, replicas - 1 + parts - 1)
-    loop(replicas - 1, lambda step: place_copy(step, me).start())
-
     zero, one = jnp.zeros((), BF16), jnp.ones((), BF16)
     count = counting(64, PAIR)
     row_freqs, column_freqs = frequencies(places)
@@ -214,8 +219,8 @@
 
     loads[1].wait()
     for index in range(quads):
-        hots = [hot(freqs[index : index + 1, :]) for freqs in (row_freqs, column_freqs)]
-        found = dot(gather_ref[...], jnp.concatenate(hots, axis=1))
+        pair = [hot(freqs[index : index + 1, :]) for freqs in (row_freqs, column_freqs)]
+        found = dot(gather_ref[...], jnp.concatenate(pair, axis=1))
         row_side[rows(index), :] = found[:64, :PAIR] + found[64:, :PAIR]
         for half in range(2):
             side = found[half * 64 : (half + 1) * 64, PAIR:]
@@ -223,6 +228,9 @@
                 column_side[pl.ds(index * QUAD + part * 64, 64), half * PAIR : (half + 1) * PAIR] = (
                     jnp.where(lanes == part, side, 0.0).astype(BF16)
                 )
+
+    pl.semaphore_wait(barrier, replicas - 1 + parts - 1)
+    loop(replicas - 1, lambda step: place_copy(step, me).start())
 
     for chunk in range(chunks):
         for load in chunk_loads(chunk):
@@ -236,15 +244,6 @@
             value_lists[me, pl.ds(line(index), 1), :] = jnp.sum(found, axis=0, keepdims=True)
         loop(replicas - 1, lambda step: value_copy(chunk, step, me).start())
 
-    for index in range(quads):
-        scaled = row_side[rows(index), :] * value_lists[me, pl.ds(line(index), 1), :]
-        high, low = split(scaled)
-        left = jnp.concatenate(
-            [jnp.concatenate([high, high], axis=1), jnp.concatenate([low, low], axis=1)], axis=0
-        )
-        back = dot_t(left, column_side[block(index), :])
-        summed[:, block(index)] = summed[:, block(index)] - (back[:64, :] + back[64:, :])
-
     def source(step):
         return lax.rem(me + replicas - step - 1, replicas)
 
@@ -256,13 +255,14 @@
             both[rows(index), half * PAIR : (half + 1) * PAIR] = part
 
     def regroup_places(group):
-        members = [
-            frequencies(place_lists[group * GROUP + member, :, :].astype(jnp.int32))
-            for member in range(GROUP)
-        ]
+        low, cell = [], []
+        for member in range(GROUP):
+            spots = place_lists[group * GROUP + member, :, :].astype(jnp.int32)
+            low.append((spots // 64 % 32).astype(F32))
+            cell.append((spots // 2048 * 64 + spots % 64).astype(F32))
         for part in range(4):
-            row_parts[group, part, :, :] = regroup([member[0] for member in members], part)
-            column_parts[group, part, :, :] = regroup([member[1] for member in members], part)
+            low_parts[group, part, :, :] = regroup(low, part)
+            cell_parts[group, part, :, :] = regroup(cell, part)
 
     def regroup_values(group, chunk):
         span = slice(chunk * tall, (chunk + 1) * tall)
@@ -271,38 +271,40 @@
             value_parts[group, part, span, :] = regroup(members, part)
 
     loop(replicas - 1, lambda step: place_copy(step, source(step)).wait_recv())
-    loop(groups, regroup_places)
-
-    count_group = counting(64, GROUP * 32)
-
-    def decode(group, index, part):
-        place = slice(line(index), line(index) + 1)
-        row_hot = flat(jnp.where(count_group == spread(row_parts[group, part, place, :]), one, zero))
-        here = count_group == spread(column_parts[group, part, place, :])
-        high, low = split(jnp.broadcast_to(value_parts[group, part, place, :], (16, GROUP * 32)))
-        right = jnp.concatenate(
-            [flat(jnp.where(here, high[None], zero)), flat(jnp.where(here, low[None], zero))], axis=0
-        )
-        result = dot_t(row_hot, right)
-        return result + pltpu.roll(result, 64, axis=1)
-
-    def decode_pair(group, index, side):
-        left, right = (decode(group, index, 2 * side + place) for place in range(2))
-        return jnp.where(lane_part(left.shape) < 2, left, right)
+    spans = 4 * quads
+    count_cell, count_low = counting(PAIR, GROUP * 32), counting(32, GROUP * 32)
+
+    def cells(group, span):
+        return pl.ds(pl.multiple_of((group * spans + span) * PAIR, PAIR), PAIR)
+
+    def mark(group):
+        regroup_places(group)
+        for span in range(spans):
+            cell = cell_parts[group, span % 4, pl.ds(line(span // 4), 1), :]
+            hots[cells(group, span), :] = flat(
+                jnp.where(count_cell == spread(cell), one, zero)
+            ).astype(F8)
+
+    def decode(group, span):
+        place = pl.ds(line(span // 4), 1)
+        here = count_low == spread(low_parts[group, span % 4, place, :])
+        halves = split(jnp.broadcast_to(value_parts[group, span % 4, place, :], (16, GROUP * 32)))
+        left = jnp.concatenate([flat(jnp.where(here, half[None], zero)) for half in halves], axis=0)
+        result = dot_t(left, hots[cells(group, span), :])
+        return result[:32, :] + result[32:, :]
+
+    each(groups, mark)
 
     square = jnp.zeros((8, PAIR), F32)
     for chunk in range(chunks):
         loop(replicas - 1, lambda step: value_copy(chunk, step, source(step)).wait_recv())
-        loop(groups, lambda group: regroup_values(group, chunk))
-        for index in range(chunk * per, (chunk + 1) * per):
-            for side in range(2):
-                total = decode_pair(0, index, side)
-                if groups > 1:
-                    total = lax.fori_loop(
-                        1, groups, lambda step, acc: acc + decode_pair(step, index, side), total
-                    )
-                square = square + jnp.sum((total * total).reshape(8, 8, PAIR), axis=0)
-                keep_pair(2 * index + side, total)
+        each(groups, lambda group: regroup_values(group, chunk))
+        for span in range(chunk * per * 4, (chunk + 1) * per * 4):
+            total = decode(0, span)
+            if groups > 1:
+                total = lax.fori_loop(1, groups, lambda step, acc: acc + decode(step, span), total)
+            square = square + jnp.sum((total * total).reshape(4, 8, PAIR), axis=0)
+            sums[pl.ds(span * 32, 32), :] = total
 
     squares[mine, :, :] = square
 
@@ -318,9 +320,23 @@
 
     for load in loads[2:4]:
         load.wait()
+    first = lane_part((32, PAIR)) < 2
+    for pair in range(2 * quads):
+        left, right = (sums[pl.ds((2 * pair + side) * 32, 32), :] for side in range(2))
+        top = jnp.where(first, left, pltpu.roll(right, 64, axis=1))
+        bottom = jnp.where(first, pltpu.roll(left, 64, axis=1), right)
+        keep_pair(pair, jnp.concatenate([top, bottom], axis=0))
     coefs[...] = column_transform(both[...], columns_ref[...])
     for index in range(quads):
         update[:, block(index)] = row_transform(rows_ref[...], quad(coefs, index))
+    for index in range(quads):
+        scaled = row_side[rows(index), :] * value_lists[me, pl.ds(line(index), 1), :]
+        high, low = split(scaled)
+        left = jnp.concatenate(
+            [jnp.concatenate([high, high], axis=1), jnp.concatenate([low, low], axis=1)], axis=0
+        )
+        back = dot_t(left, column_side[block(index), :])
+        summed[:, block(index)] = summed[:, block(index)] - (back[:64, :] + back[64:, :])
 
     loads[4].wait()
     loop(replicas - 1, lambda step: place_copy(step, me).wait_send())
@@ -381,6 +397,8 @@
             pltpu.VMEM((groups, 4, listed, GROUP * 32), F32),
             pltpu.VMEM((groups, 4, listed, GROUP * 32), F32),
             pltpu.VMEM((groups, 4, listed, GROUP * 32), F32),
+            pltpu.VMEM((groups * 4 * quads * PAIR, GROUP * 32), F8),
+            pltpu.VMEM((4 * quads * 32, PAIR), F32),
             pltpu.SemaphoreType.DMA((5,)),
             pltpu.SemaphoreType.DMA((chunks, 2)),
             pltpu.SemaphoreType.DMA((replicas,)),
@@ -391,7 +409,7 @@
             pltpu.SemaphoreType.DMA((parts,)),
         ],
         compiler_params=pltpu.CompilerParams(
-            collective_id=0, has_side_effects=True, vmem_limit_bytes=24 * 1024 * 1024
+            collective_id=0, has_side_effects=True, vmem_limit_bytes=(22 + 2 * groups) * 1024 * 1024
         ),
     )(
         *(

time: 17.3 us -> 16 us (0.925)
  Pallas kernels: 16.4 us -> 15.2 us
    pallas_call x1, Pallas kernels: 15.1 us -> 13.9 us  [local(): pl.pallas_call(functools.partial(kernel, replicas, parts, chunks), out_sh...]
where the time goes in v2:
time: 16 us; the launch traced here: 15.8 us
  Pallas kernels  15.2 us (95%)
  between operations  0.64 us (4%)
    pallas_call x1, Pallas kernels, local(): pl.pallas_call(functools.partial(kernel, replicas, parts, chunks), out_sh...  13.9 us
    pallas_call x1, Pallas kernels, local(): pl.pallas_call(functools.partial(deliver, chunks, float(height * width *...  1.24 us

profile of v2, /device:TPU:0, one launch (start us, length us, event | category | flops | bytes accessed | tf_op | source)
XLA Modules:
  0.0 15.8 jit_solution(3862925030638733309)
XLA Ops:
  0.6 13.9 %shard_map.86 = (f32[64,3584]{1,0:T(8,128)S(1)}, f32[64,3584]{1,0:T(8,128)S(1)}, f32[64,3584]{1,0:T(8,128)S(1)}, f32[4,8,128]{2,1,0:T(8,128)S(1)}) custom-call(bf16[1,64,3584]{2,1,0:T(8,128)(2,1)} %gradient_ref.1, f32[1,64,3584]{2,1,0:T(8,128)} %momentum_ref.1, f32[64,3584]{1,0:T(8,128)} %weights_ref.1, s32[1,1,32,56]{3,2,1,0:T(8,128)} %bitcast.1, ...), custom_call_target="tpu_custom_call" | custom-call | tf_op jit(solution)/shard_map/pallas_call | solution.py:380
  14.6 1.2 %shard_map.87 = (f32[1,64,3584]{2,1,0:T(8,128)}, f32[64,3584]{1,0:T(8,128)}) custom-call(f32[64,3584]{1,0:T(8,128)S(1)} %get-tuple-element.6.summed, f32[64,3584]{1,0:T(8,128)S(1)} %get-tuple-element.7.update, f32[64,3584]{1,0:T(8,128)S(1)} %get-tuple-element.8.weights, f32[4,8,128]{2,1,0:T(8,128)S(1)} %get-tuple-element.9.squares), custom_call_target="tpu_custom_call" | custom-call | tf_op jit(solution)/shard_map/pallas_call | solution.py:422

commit v3 on v2

--- a/solution.py
+++ b/solution.py
@@ -33,7 +33,7 @@
 def side_tables():
     table = dct_table()
     high, low = halves(table.T)
-    gather = np.concatenate([high, low], axis=0)
+    gather = np.concatenate([high, low], axis=1)
     rows = np.concatenate([high, low, high, low], axis=1)
     columns = np.concatenate(halves(np.kron(np.eye(2), table)), axis=1)
     return gather, rows, columns
@@ -86,14 +86,27 @@
 def regroup(members, part):
     result = []
     for start in range(0, GROUP, 4):
-        joined = None
-        for place in range(4):
-            member = members[start + place]
-            shift = (place - part) % 4 * 32
-            moved = pltpu.roll(member, shift, axis=1) if shift else member
-            joined = moved if joined is None else jnp.where(lane_part(moved.shape) == place, moved, joined)
+        joined = members[start + -part % 4]
+        for place in range(1, 4):
+            member = members[start + (place - part) % 4]
+            joined = jnp.where(lane_part(joined.shape) == place, member, joined)
         result.append(joined)
     return jnp.concatenate(result, axis=1)
+
+
+def partners(me, count):
+    if count > 16 or count & (count - 1):
+        return (
+            lambda step: lax.rem(me + step + 1, count),
+            lambda step: lax.rem(me + count - step - 1, count),
+        )
+    bits = [1 << bit for bit in range(count.bit_length() - 1)]
+    flips = {bit: bit * (1 - 2 * lax.rem(me // bit, 2)) for bit in bits}
+
+    def across(step):
+        return me + sum(flips[bit] for bit in bits if (count - 1 - step) & bit)
+
+    return across, across
 
 
 def loop(count, body):
@@ -159,16 +172,18 @@
         load.start()
 
     barrier = pltpu.get_barrier_semaphore()
+    replica, source = partners(me, replicas)
+    other_part, part_source = partners(mine, parts)
 
     def greet_replica(step):
         pl.semaphore_signal(
-            barrier, inc=1, device_id={"dp": lax.rem(me + step + 1, replicas)},
+            barrier, inc=1, device_id={"dp": replica(step)},
             device_id_type=pl.DeviceIdType.MESH,
         )
 
     def greet_part(step):
         pl.semaphore_signal(
-            barrier, inc=1, device_id={"mp": lax.rem(mine + step + 1, parts)},
+            barrier, inc=1, device_id={"mp": other_part(step)},
             device_id_type=pl.DeviceIdType.MESH,
         )
 
@@ -179,7 +194,7 @@
         return pltpu.make_async_remote_copy(
             src_ref=lists.at[slot, span], dst_ref=lists.at[slot, span],
             send_sem=send_sem, recv_sem=recv_sem,
-            device_id={"dp": lax.rem(me + step + 1, replicas)},
+            device_id={"dp": replica(step)},
             device_id_type=pl.DeviceIdType.MESH,
         )
 
@@ -201,8 +216,9 @@
 
     loads[0].wait()
     flipped[...] = jnp.transpose(places_ref[...])
+    turn = lax.rem(me, 4)
     places = jnp.concatenate(
-        [flipped[pl.ds(part, quads, stride=4), :] for part in range(4)], axis=1
+        [flipped[pl.ds(lax.rem(place + 4 - turn, 4), quads, stride=4), :] for place in range(4)], axis=1
     )
     for chunk in range(chunks):
         place_lists[me, chunk * tall : chunk * tall + per, :] = places[
@@ -212,7 +228,7 @@
     zero, one = jnp.zeros((), BF16), jnp.ones((), BF16)
     count = counting(64, PAIR)
     row_freqs, column_freqs = frequencies(places)
-    lanes = lane_part((64, PAIR))
+    lanes = lax.rem(lane_part((64, PAIR)) + 4 - turn, 4)
 
     def hot(row):
         return flat(jnp.where(count == spread(row), one, zero))
@@ -220,13 +236,13 @@
     loads[1].wait()
     for index in range(quads):
         pair = [hot(freqs[index : index + 1, :]) for freqs in (row_freqs, column_freqs)]
-        found = dot(gather_ref[...], jnp.concatenate(pair, axis=1))
-        row_side[rows(index), :] = found[:64, :PAIR] + found[64:, :PAIR]
-        for half in range(2):
-            side = found[half * 64 : (half + 1) * 64, PAIR:]
+        both_hot = jnp.concatenate(pair, axis=1)
+        found = dot(gather_ref[...], jnp.concatenate([both_hot, both_hot], axis=0))
+        row_side[rows(index), :] = found[:, :PAIR]
+        for half, side in enumerate(split(found[:, PAIR:])):
             for part in range(4):
                 column_side[pl.ds(index * QUAD + part * 64, 64), half * PAIR : (half + 1) * PAIR] = (
-                    jnp.where(lanes == part, side, 0.0).astype(BF16)
+                    jnp.where(lanes == part, side, zero)
                 )
 
     pl.semaphore_wait(barrier, replicas - 1 + parts - 1)
@@ -244,9 +260,6 @@
             value_lists[me, pl.ds(line(index), 1), :] = jnp.sum(found, axis=0, keepdims=True)
         loop(replicas - 1, lambda step: value_copy(chunk, step, me).start())
 
-    def source(step):
-        return lax.rem(me + replicas - step - 1, replicas)
-
     def quad(ref, index):
         return jnp.concatenate([ref[rows(2 * index), :], ref[rows(2 * index + 1), :]], axis=1)
 
@@ -312,7 +325,7 @@
         return pltpu.make_async_remote_copy(
             src_ref=squares.at[slot], dst_ref=squares.at[slot],
             send_sem=square_send.at[step], recv_sem=square_recv.at[slot],
-            device_id={"mp": lax.rem(mine + step + 1, parts)},
+            device_id={"mp": other_part(step)},
             device_id_type=pl.DeviceIdType.MESH,
         )
 
@@ -345,7 +358,7 @@
     loop(parts - 1, lambda step: square_copy(step, mine).wait_send())
     loop(
         parts - 1,
-        lambda step: square_copy(step, lax.rem(mine + parts - step - 1, parts)).wait_recv(),
+        lambda step: square_copy(step, part_source(step)).wait_recv(),
     )
 
 

time: 16 us -> 16.4 us (1.025)
  Pallas kernels: 15.2 us -> 15.5 us
    pallas_call x1, Pallas kernels: 13.9 us -> 14.2 us  [local(): pl.pallas_call(functools.partial(kernel, replicas, parts, chunks), out_sh...]
where the time goes in v3:
time: 16.4 us; the launch traced here: 16.1 us
  Pallas kernels  15.5 us (95%)
  between operations  0.64 us (4%)
    pallas_call x1, Pallas kernels, local(): pl.pallas_call(functools.partial(kernel, replicas, parts, chunks), out_sh...  14.2 us
    pallas_call x1, Pallas kernels, local(): pl.pallas_call(functools.partial(deliver, chunks, float(height * width *...  1.24 us

profile of v3, /device:TPU:0, one launch (start us, length us, event | category | flops | bytes accessed | tf_op | source)
XLA Modules:
  0.0 16.1 jit_solution(14105813652215597607)
XLA Ops:
  0.6 14.2 %shard_map.86 = (f32[64,3584]{1,0:T(8,128)S(1)}, f32[64,3584]{1,0:T(8,128)S(1)}, f32[64,3584]{1,0:T(8,128)S(1)}, f32[4,8,128]{2,1,0:T(8,128)S(1)}) custom-call(bf16[1,64,3584]{2,1,0:T(8,128)(2,1)} %gradient_ref.1, f32[1,64,3584]{2,1,0:T(8,128)} %momentum_ref.1, f32[64,3584]{1,0:T(8,128)} %weights_ref.1, s32[1,1,32,56]{3,2,1,0:T(8,128)} %bitcast.1, ...), custom_call_target="tpu_custom_call" | custom-call | tf_op jit(solution)/shard_map/pallas_call | solution.py:393
  14.9 1.2 %shard_map.87 = (f32[1,64,3584]{2,1,0:T(8,128)}, f32[64,3584]{1,0:T(8,128)}) custom-call(f32[64,3584]{1,0:T(8,128)S(1)} %get-tuple-element.6.summed, f32[64,3584]{1,0:T(8,128)S(1)} %get-tuple-element.7.update, f32[64,3584]{1,0:T(8,128)S(1)} %get-tuple-element.8.weights, f32[4,8,128]{2,1,0:T(8,128)S(1)} %get-tuple-element.9.squares), custom_call_target="tpu_custom_call" | custom-call | tf_op jit(solution)/shard_map/pallas_call | solution.py:435

commit v4 on v3

--- a/solution.py
+++ b/solution.py
@@ -36,7 +36,7 @@
     gather = np.concatenate([high, low], axis=1)
     rows = np.concatenate([high, low, high, low], axis=1)
     columns = np.concatenate(halves(np.kron(np.eye(2), table)), axis=1)
-    return gather, rows, columns
+    return gather, np.concatenate([rows, columns], axis=0)
 
 
 def split(value):
@@ -94,19 +94,8 @@
     return jnp.concatenate(result, axis=1)
 
 
-def partners(me, count):
-    if count > 16 or count & (count - 1):
-        return (
-            lambda step: lax.rem(me + step + 1, count),
-            lambda step: lax.rem(me + count - step - 1, count),
-        )
-    bits = [1 << bit for bit in range(count.bit_length() - 1)]
-    flips = {bit: bit * (1 - 2 * lax.rem(me // bit, 2)) for bit in bits}
-
-    def across(step):
-        return me + sum(flips[bit] for bit in bits if (count - 1 - step) & bit)
-
-    return across, across
+def partner(me, count, step):
+    return step + (step - me + count) // count
 
 
 def loop(count, body):
@@ -126,11 +115,11 @@
 
 def kernel(
     replicas, parts, chunks,
-    gradient_ref, momentum_ref, weights_ref, places_hbm, gather_hbm, rows_hbm, columns_hbm,
+    gradient_ref, momentum_ref, weights_ref, places_hbm, gather_hbm, tables_hbm,
     summed, update, wts, squares,
-    grad, mom, places_ref, gather_ref, rows_ref, columns_ref, flipped, row_side, column_side, both, coefs,
+    grad, mom, places_ref, gather_ref, tables_ref, flipped, row_side, column_side, both, coefs,
     place_lists, value_lists, low_parts, cell_parts, value_parts, hots, sums,
-    in_sem, chunk_sem, place_send, place_recv, value_send, value_recv, square_send, square_recv,
+    in_sem, chunk_sem, place_sem, value_sem, square_sem,
 ):
     me, mine = lax.axis_index("dp"), lax.axis_index("mp")
     width = summed.shape[1]
@@ -159,7 +148,7 @@
         for index, (source, target) in enumerate(
             (
                 (places_hbm.at[0, 0], places_ref), (gather_hbm, gather_ref),
-                (rows_hbm, rows_ref), (columns_hbm, columns_ref), (weights_ref, wts),
+                (tables_hbm, tables_ref), (weights_ref, wts),
             )
         )
     ]
@@ -168,12 +157,10 @@
     for chunk in range(chunks):
         for load in chunk_loads(chunk):
             load.start()
-    for load in loads[2:]:
-        load.start()
 
     barrier = pltpu.get_barrier_semaphore()
-    replica, source = partners(me, replicas)
-    other_part, part_source = partners(mine, parts)
+    replica = functools.partial(partner, me, replicas)
+    other_part = functools.partial(partner, mine, parts)
 
     def greet_replica(step):
         pl.semaphore_signal(
@@ -190,24 +177,20 @@
     loop(replicas - 1, greet_replica)
     loop(parts - 1, greet_part)
 
-    def list_copy(lists, send_sem, recv_sem, step, slot, span):
+    def list_copy(lists, sems, step, slot, span):
         return pltpu.make_async_remote_copy(
             src_ref=lists.at[slot, span], dst_ref=lists.at[slot, span],
-            send_sem=send_sem, recv_sem=recv_sem,
-            device_id={"dp": replica(step)},
-            device_id_type=pl.DeviceIdType.MESH,
+            send_sem=sems.at[0], recv_sem=sems.at[1],
+            device_id={"dp": replica(step)}, device_id_type=pl.DeviceIdType.MESH,
         )
 
     def place_copy(step, slot):
-        return list_copy(
-            place_lists, place_send.at[step], place_recv.at[slot], step, slot, pl.ds(0, chunks * tall)
-        )
+        return list_copy(place_lists, place_sem, step, slot, pl.ds(0, (chunks - 1) * tall + per))
 
     def value_copy(chunk, step, slot):
-        return list_copy(
-            value_lists, value_send.at[chunk, step], value_recv.at[chunk, slot],
-            step, slot, pl.ds(chunk * tall, tall),
-        )
+        return list_copy(value_lists, value_sem.at[chunk], step, slot, pl.ds(chunk * tall, per))
+
+    others = pl.ds(0, replicas - 1)
 
     groups = place_lists.shape[0] // GROUP
     for slot in range(replicas, groups * GROUP):
@@ -259,6 +242,8 @@
             found = (found[:, :PAIR] + found[:, PAIR:]) * row_side[rows(index), :]
             value_lists[me, pl.ds(line(index), 1), :] = jnp.sum(found, axis=0, keepdims=True)
         loop(replicas - 1, lambda step: value_copy(chunk, step, me).start())
+    for load in loads[2:]:
+        load.start()
 
     def quad(ref, index):
         return jnp.concatenate([ref[rows(2 * index), :], ref[rows(2 * index + 1), :]], axis=1)
@@ -283,7 +268,7 @@
         for part in range(4):
             value_parts[group, part, span, :] = regroup(members, part)
 
-    loop(replicas - 1, lambda step: place_copy(step, source(step)).wait_recv())
+    place_copy(0, others).wait_recv()
     spans = 4 * quads
     count_cell, count_low = counting(PAIR, GROUP * 32), counting(32, GROUP * 32)
 
@@ -310,7 +295,7 @@
 
     square = jnp.zeros((8, PAIR), F32)
     for chunk in range(chunks):
-        loop(replicas - 1, lambda step: value_copy(chunk, step, source(step)).wait_recv())
+        value_copy(chunk, 0, others).wait_recv()
         each(groups, lambda group: regroup_values(group, chunk))
         for span in range(chunk * per * 4, (chunk + 1) * per * 4):
             total = decode(0, span)
@@ -319,29 +304,27 @@
             square = square + jnp.sum((total * total).reshape(4, 8, PAIR), axis=0)
             sums[pl.ds(span * 32, 32), :] = total
 
-    squares[mine, :, :] = square
+    squares[mine, 0:1, :] = jnp.sum(square, axis=0, keepdims=True)
 
     def square_copy(step, slot):
         return pltpu.make_async_remote_copy(
-            src_ref=squares.at[slot], dst_ref=squares.at[slot],
-            send_sem=square_send.at[step], recv_sem=square_recv.at[slot],
-            device_id={"mp": other_part(step)},
-            device_id_type=pl.DeviceIdType.MESH,
+            src_ref=squares.at[slot, pl.ds(0, 1)], dst_ref=squares.at[slot, pl.ds(0, 1)],
+            send_sem=square_sem.at[0], recv_sem=square_sem.at[1],
+            device_id={"mp": other_part(step)}, device_id_type=pl.DeviceIdType.MESH,
         )
 
     loop(parts - 1, lambda step: square_copy(step, mine).start())
 
-    for load in loads[2:4]:
-        load.wait()
+    loads[2].wait()
     first = lane_part((32, PAIR)) < 2
     for pair in range(2 * quads):
         left, right = (sums[pl.ds((2 * pair + side) * 32, 32), :] for side in range(2))
         top = jnp.where(first, left, pltpu.roll(right, 64, axis=1))
         bottom = jnp.where(first, pltpu.roll(left, 64, axis=1), right)
         keep_pair(pair, jnp.concatenate([top, bottom], axis=0))
-    coefs[...] = column_transform(both[...], columns_ref[...])
+    coefs[...] = column_transform(both[...], tables_ref[64:, :])
     for index in range(quads):
-        update[:, block(index)] = row_transform(rows_ref[...], quad(coefs, index))
+        update[:, block(index)] = row_transform(tables_ref[:64, :], quad(coefs, index))
     for index in range(quads):
         scaled = row_side[rows(index), :] * value_lists[me, pl.ds(line(index), 1), :]
         high, low = split(scaled)
@@ -351,22 +334,18 @@
         back = dot_t(left, column_side[block(index), :])
         summed[:, block(index)] = summed[:, block(index)] - (back[:64, :] + back[64:, :])
 
-    loads[4].wait()
-    loop(replicas - 1, lambda step: place_copy(step, me).wait_send())
-    for chunk in range(chunks):
-        loop(replicas - 1, lambda step: value_copy(chunk, step, me).wait_send())
-    loop(parts - 1, lambda step: square_copy(step, mine).wait_send())
-    loop(
-        parts - 1,
-        lambda step: square_copy(step, part_source(step)).wait_recv(),
-    )
+    loads[3].wait()
+    place_copy(0, others).wait_send()
+    for chunk in range(chunks):
+        value_copy(chunk, 0, others).wait_send()
+    square_copy(0, pl.ds(0, parts - 1)).wait()
 
 
 def deliver(chunks, entries, summed, update, weights, squares, out_momentum_ref, out_weights_ref, result, out_sem):
     share = weights.shape[1] // chunks
     first = pltpu.make_async_copy(summed, out_momentum_ref.at[0], out_sem.at[chunks])
     first.start()
-    meansq = jnp.sum(jnp.sum(squares[...], axis=0)) / entries
+    meansq = jnp.sum(squares[:, 0, :]) / entries
     factor = lax.rsqrt(jnp.full((1, share), meansq + 1.0, F32))
     stores = []
     for chunk in range(chunks):
@@ -393,7 +372,7 @@
     results = pl.pallas_call(
         functools.partial(kernel, replicas, parts, chunks),
         out_shape=(wide, wide, wide, jax.ShapeDtypeStruct((parts, 8, PAIR), F32)),
-        in_specs=[pl.BlockSpec(memory_space=pltpu.HBM)] * 7,
+        in_specs=[pl.BlockSpec(memory_space=pltpu.HBM)] * 6,
         out_specs=(vmem,) * 4,
         scratch_shapes=[
             pltpu.VMEM((height, width), BF16),
@@ -412,14 +391,11 @@
             pltpu.VMEM((groups, 4, listed, GROUP * 32), F32),
             pltpu.VMEM((groups * 4 * quads * PAIR, GROUP * 32), F8),
             pltpu.VMEM((4 * quads * 32, PAIR), F32),
-            pltpu.SemaphoreType.DMA((5,)),
+            pltpu.SemaphoreType.DMA((4,)),
             pltpu.SemaphoreType.DMA((chunks, 2)),
-            pltpu.SemaphoreType.DMA((replicas,)),
-            pltpu.SemaphoreType.DMA((replicas,)),
-            pltpu.SemaphoreType.DMA((chunks, replicas)),
-            pltpu.SemaphoreType.DMA((chunks, replicas)),
-            pltpu.SemaphoreType.DMA((parts,)),
-            pltpu.SemaphoreType.DMA((parts,)),
+            pltpu.SemaphoreType.DMA((2,)),
+            pltpu.SemaphoreType.DMA((chunks, 2)),
+            pltpu.SemaphoreType.DMA((2,)),
         ],
         compiler_params=pltpu.CompilerParams(
             collective_id=0, has_side_effects=True, vmem_limit_bytes=(22 + 2 * groups) * 1024 * 1024

time: 16.4 us -> 15.4 us (0.939)
  Pallas kernels: 15.5 us -> 14.6 us
    pallas_call x1, Pallas kernels: 14.2 us -> 13.3 us  [local(): pl.pallas_call(functools.partial(kernel, replicas, parts, chunks), out_sh...]
where the time goes in v4:
time: 15.4 us; the launch traced here: 15.2 us
  Pallas kernels  14.6 us (95%)
  between operations  0.64 us (4%)
    pallas_call x1, Pallas kernels, local(): pl.pallas_call(functools.partial(kernel, replicas, parts, chunks), out_sh...  13.3 us
    pallas_call x1, Pallas kernels, local(): pl.pallas_call(functools.partial(deliver, chunks, float(height * width *...  1.24 us

profile of v4, /device:TPU:0, one launch (start us, length us, event | category | flops | bytes accessed | tf_op | source)
XLA Modules:
  0.0 15.2 jit_solution(251489985080545144)
XLA Ops:
  0.6 13.3 %shard_map.77 = (f32[64,3584]{1,0:T(8,128)S(1)}, f32[64,3584]{1,0:T(8,128)S(1)}, f32[64,3584]{1,0:T(8,128)S(1)}, f32[4,8,128]{2,1,0:T(8,128)S(1)}) custom-call(bf16[1,64,3584]{2,1,0:T(8,128)(2,1)} %gradient_ref.1, f32[1,64,3584]{2,1,0:T(8,128)} %momentum_ref.1, f32[64,3584]{1,0:T(8,128)} %weights_ref.1, s32[1,1,32,56]{3,2,1,0:T(8,128)} %bitcast.1, ...), custom_call_target="tpu_custom_call" | custom-call | tf_op jit(solution)/shard_map/pallas_call | solution.py:372
  14.0 1.2 %shard_map.78 = (f32[1,64,3584]{2,1,0:T(8,128)}, f32[64,3584]{1,0:T(8,128)}) custom-call(f32[64,3584]{1,0:T(8,128)S(1)} %get-tuple-element.6.summed, f32[64,3584]{1,0:T(8,128)S(1)} %get-tuple-element.7.update, f32[64,3584]{1,0:T(8,128)S(1)} %get-tuple-element.8.weights, f32[4,8,128]{2,1,0:T(8,128)S(1)} %get-tuple-element.9.squares), custom_call_target="tpu_custom_call" | custom-call | tf_op jit(solution)/shard_map/pallas_call | solution.py:411

commit v5 on v4

--- a/solution.py
+++ b/solution.py
@@ -117,7 +117,7 @@
     replicas, parts, chunks,
     gradient_ref, momentum_ref, weights_ref, places_hbm, gather_hbm, tables_hbm,
     summed, update, wts, squares,
-    grad, mom, places_ref, gather_ref, tables_ref, flipped, row_side, column_side, both, coefs,
+    grad, mom, places_ref, gather_ref, tables_ref, flipped, row_side, column_high, column_low, both, coefs,
     place_lists, value_lists, low_parts, cell_parts, value_parts, hots, sums,
     in_sem, chunk_sem, place_sem, value_sem, square_sem,
 ):
@@ -174,7 +174,7 @@
             device_id_type=pl.DeviceIdType.MESH,
         )
 
-    loop(replicas - 1, greet_replica)
+    loop(replicas - 1, lambda step: greet_replica(replicas - 2 - step))
     loop(parts - 1, greet_part)
 
     def list_copy(lists, sems, step, slot, span):
@@ -208,13 +208,23 @@
             chunk * per : (chunk + 1) * per
         ].astype(F32)
 
+    pl.semaphore_wait(barrier, replicas - 1 + parts - 1)
+    loop(replicas - 1, lambda step: place_copy(step, me).start())
+
     zero, one = jnp.zeros((), BF16), jnp.ones((), BF16)
     count = counting(64, PAIR)
     row_freqs, column_freqs = frequencies(places)
-    lanes = lax.rem(lane_part((64, PAIR)) + 4 - turn, 4)
+    lanes = lax.rem(lane_part((64, QUAD)) + 4 - turn, 4)
 
     def hot(row):
         return flat(jnp.where(count == spread(row), one, zero))
+
+    def total(index):
+        return 0.9 * mom[:, block(index)] + grad[:, block(index)].astype(F32)
+
+    def column_side(index):
+        side = jnp.concatenate([column_high[rows(index), :], column_low[rows(index), :]], axis=1)
+        return jnp.concatenate([jnp.where(lanes == part, side, zero) for part in range(4)], axis=0)
 
     loads[1].wait()
     for index in range(quads):
@@ -222,22 +232,13 @@
         both_hot = jnp.concatenate(pair, axis=1)
         found = dot(gather_ref[...], jnp.concatenate([both_hot, both_hot], axis=0))
         row_side[rows(index), :] = found[:, :PAIR]
-        for half, side in enumerate(split(found[:, PAIR:])):
-            for part in range(4):
-                column_side[pl.ds(index * QUAD + part * 64, 64), half * PAIR : (half + 1) * PAIR] = (
-                    jnp.where(lanes == part, side, zero)
-                )
-
-    pl.semaphore_wait(barrier, replicas - 1 + parts - 1)
-    loop(replicas - 1, lambda step: place_copy(step, me).start())
+        column_high[rows(index), :], column_low[rows(index), :] = split(found[:, PAIR:])
 
     for chunk in range(chunks):
         for load in chunk_loads(chunk):
             load.wait()
         for index in range(chunk * per, (chunk + 1) * per):
-            value = 0.9 * mom[:, block(index)] + grad[:, block(index)].astype(F32)
-            summed[:, block(index)] = value
-            found = dot(jnp.concatenate(split(value), axis=0), column_side[block(index), :])
+            found = dot(jnp.concatenate(split(total(index)), axis=0), column_side(index))
             found = found[:64, :] + found[64:, :]
             found = (found[:, :PAIR] + found[:, PAIR:]) * row_side[rows(index), :]
             value_lists[me, pl.ds(line(index), 1), :] = jnp.sum(found, axis=0, keepdims=True)
@@ -298,11 +299,11 @@
         value_copy(chunk, 0, others).wait_recv()
         each(groups, lambda group: regroup_values(group, chunk))
         for span in range(chunk * per * 4, (chunk + 1) * per * 4):
-            total = decode(0, span)
+            cells_sum = decode(0, span)
             if groups > 1:
-                total = lax.fori_loop(1, groups, lambda step, acc: acc + decode(step, span), total)
-            square = square + jnp.sum((total * total).reshape(4, 8, PAIR), axis=0)
-            sums[pl.ds(span * 32, 32), :] = total
+                cells_sum = lax.fori_loop(1, groups, lambda step, acc: acc + decode(step, span), cells_sum)
+            square = square + jnp.sum((cells_sum * cells_sum).reshape(4, 8, PAIR), axis=0)
+            sums[pl.ds(span * 32, 32), :] = cells_sum
 
     squares[mine, 0:1, :] = jnp.sum(square, axis=0, keepdims=True)
 
@@ -331,8 +332,8 @@
         left = jnp.concatenate(
             [jnp.concatenate([high, high], axis=1), jnp.concatenate([low, low], axis=1)], axis=0
         )
-        back = dot_t(left, column_side[block(index), :])
-        summed[:, block(index)] = summed[:, block(index)] - (back[:64, :] + back[64:, :])
+        back = dot_t(left, column_side(index))
+        summed[:, block(index)] = total(index) - (back[:64, :] + back[64:, :])
 
     loads[3].wait()
     place_copy(0, others).wait_send()
@@ -381,7 +382,8 @@
             *[pltpu.VMEM(table.shape, BF16) for table in tables],
             pltpu.VMEM((4 * quads, entries), jnp.int32),
             pltpu.VMEM((quads * 64, PAIR), F32),
-            pltpu.VMEM((quads * QUAD, QUAD), BF16),
+            pltpu.VMEM((quads * 64, PAIR), BF16),
+            pltpu.VMEM((quads * 64, PAIR), BF16),
             pltpu.VMEM((2 * quads * 64, QUAD), BF16),
             pltpu.VMEM((2 * quads * 64, PAIR), F32),
             pltpu.VMEM((groups * GROUP, listed, PAIR), F32),

time: 15.4 us -> 15.4 us (level)
  no operation moved by 1% of the time
where the time goes in v5:
time: 15.4 us; the launch traced here: 15.1 us
  Pallas kernels  14.5 us (94%)
  between operations  0.64 us (4%)
    pallas_call x1, Pallas kernels, local(): pl.pallas_call(functools.partial(kernel, replicas, parts, chunks), out_sh...  13.3 us
    pallas_call x1, Pallas kernels, local(): pl.pallas_call(functools.partial(deliver, chunks, float(height * width *...  1.24 us

profile of v5, /device:TPU:0, one launch (start us, length us, event | category | flops | bytes accessed | tf_op | source)
XLA Modules:
  0.0 15.1 jit_solution(17113711454403218372)
XLA Ops:
  0.6 13.3 %shard_map.77 = (f32[64,3584]{1,0:T(8,128)S(1)}, f32[64,3584]{1,0:T(8,128)S(1)}, f32[64,3584]{1,0:T(8,128)S(1)}, f32[4,8,128]{2,1,0:T(8,128)S(1)}) custom-call(bf16[1,64,3584]{2,1,0:T(8,128)(2,1)} %gradient_ref.1, f32[1,64,3584]{2,1,0:T(8,128)} %momentum_ref.1, f32[64,3584]{1,0:T(8,128)} %weights_ref.1, s32[1,1,32,56]{3,2,1,0:T(8,128)} %bitcast.1, ...), custom_call_target="tpu_custom_call" | custom-call | tf_op jit(solution)/shard_map/pallas_call | solution.py:373
  13.9 1.2 %shard_map.78 = (f32[1,64,3584]{2,1,0:T(8,128)}, f32[64,3584]{1,0:T(8,128)}) custom-call(f32[64,3584]{1,0:T(8,128)S(1)} %get-tuple-element.6.summed, f32[64,3584]{1,0:T(8,128)S(1)} %get-tuple-element.7.update, f32[64,3584]{1,0:T(8,128)S(1)} %get-tuple-element.8.weights, f32[4,8,128]{2,1,0:T(8,128)S(1)} %get-tuple-element.9.squares), custom_call_target="tpu_custom_call" | custom-call | tf_op jit(solution)/shard_map/pallas_call | solution.py:413

commit v6 on v5

--- a/solution.py
+++ b/solution.py
@@ -12,6 +12,7 @@
 PAIR = 128
 GROUP = 8
 CHUNKS = 1
+EARLY = 1
 F32 = jnp.float32
 BF16 = jnp.bfloat16
 F8 = jnp.float8_e4m3fn
@@ -209,7 +210,8 @@
         ].astype(F32)
 
     pl.semaphore_wait(barrier, replicas - 1 + parts - 1)
-    loop(replicas - 1, lambda step: place_copy(step, me).start())
+    early = min(replicas - 1, EARLY)
+    loop(early, lambda step: place_copy(step, me).start())
 
     zero, one = jnp.zeros((), BF16), jnp.ones((), BF16)
     count = counting(64, PAIR)
@@ -242,7 +244,10 @@
             found = found[:64, :] + found[64:, :]
             found = (found[:, :PAIR] + found[:, PAIR:]) * row_side[rows(index), :]
             value_lists[me, pl.ds(line(index), 1), :] = jnp.sum(found, axis=0, keepdims=True)
-        loop(replicas - 1, lambda step: value_copy(chunk, step, me).start())
+        loop(early, lambda step: value_copy(chunk, step, me).start())
+        if chunk == 0:
+            loop(replicas - 1 - early, lambda step: place_copy(step + early, me).start())
+        loop(replicas - 1 - early, lambda step: value_copy(chunk, step + early, me).start())
     for load in loads[2:]:
         load.start()
 

time: 15.4 us -> 15.4 us (level)
  no operation moved by 1% of the time
where the time goes in v6:
time: 15.4 us; the launch traced here: 15.1 us
  Pallas kernels  14.5 us (94%)
  between operations  0.64 us (4%)
    pallas_call x1, Pallas kernels, local(): pl.pallas_call(functools.partial(kernel, replicas, parts, chunks), out_sh...  13.3 us
    pallas_call x1, Pallas kernels, local(): pl.pallas_call(functools.partial(deliver, chunks, float(height * width *...  1.24 us

profile of v6, /device:TPU:0, one launch (start us, length us, event | category | flops | bytes accessed | tf_op | source)
XLA Modules:
  0.0 15.1 jit_solution(10136707662529198779)
XLA Ops:
  0.6 13.3 %shard_map.77 = (f32[64,3584]{1,0:T(8,128)S(1)}, f32[64,3584]{1,0:T(8,128)S(1)}, f32[64,3584]{1,0:T(8,128)S(1)}, f32[4,8,128]{2,1,0:T(8,128)S(1)}) custom-call(bf16[1,64,3584]{2,1,0:T(8,128)(2,1)} %gradient_ref.1, f32[1,64,3584]{2,1,0:T(8,128)} %momentum_ref.1, f32[64,3584]{1,0:T(8,128)} %weights_ref.1, s32[1,1,32,56]{3,2,1,0:T(8,128)} %bitcast.1, ...), custom_call_target="tpu_custom_call" | custom-call | tf_op jit(solution)/shard_map/pallas_call | solution.py:378
  13.9 1.2 %shard_map.78 = (f32[1,64,3584]{2,1,0:T(8,128)}, f32[64,3584]{1,0:T(8,128)}) custom-call(f32[64,3584]{1,0:T(8,128)S(1)} %get-tuple-element.6.summed, f32[64,3584]{1,0:T(8,128)S(1)} %get-tuple-element.7.update, f32[64,3584]{1,0:T(8,128)S(1)} %get-tuple-element.8.weights, f32[4,8,128]{2,1,0:T(8,128)S(1)} %get-tuple-element.9.squares), custom_call_target="tpu_custom_call" | custom-call | tf_op jit(solution)/shard_map/pallas_call | solution.py:418

commit v7 on v6

--- a/solution.py
+++ b/solution.py
@@ -155,9 +155,6 @@
     ]
     for load in loads[:2]:
         load.start()
-    for chunk in range(chunks):
-        for load in chunk_loads(chunk):
-            load.start()
 
     barrier = pltpu.get_barrier_semaphore()
     replica = functools.partial(partner, me, replicas)
@@ -177,6 +174,9 @@
 
     loop(replicas - 1, lambda step: greet_replica(replicas - 2 - step))
     loop(parts - 1, greet_part)
+    for chunk in range(chunks):
+        for load in chunk_loads(chunk):
+            load.start()
 
     def list_copy(lists, sems, step, slot, span):
         return pltpu.make_async_remote_copy(

time: 15.4 us -> 15.4 us (level)
  no operation moved by 1% of the time
where the time goes in v7:
time: 15.4 us; the launch traced here: 15.2 us
  Pallas kernels  14.5 us (94%)
  between operations  0.64 us (4%)
    pallas_call x1, Pallas kernels, local(): pl.pallas_call(functools.partial(kernel, replicas, parts, chunks), out_sh...  13.3 us
    pallas_call x1, Pallas kernels, local(): pl.pallas_call(functools.partial(deliver, chunks, float(height * width *...  1.24 us

profile of v7, /device:TPU:0, one launch (start us, length us, event | category | flops | bytes accessed | tf_op | source)
XLA Modules:
  0.0 15.2 jit_solution(4666049732514349355)
XLA Ops:
  0.6 13.3 %shard_map.77 = (f32[64,3584]{1,0:T(8,128)S(1)}, f32[64,3584]{1,0:T(8,128)S(1)}, f32[64,3584]{1,0:T(8,128)S(1)}, f32[4,8,128]{2,1,0:T(8,128)S(1)}) custom-call(bf16[1,64,3584]{2,1,0:T(8,128)(2,1)} %gradient_ref.1, f32[1,64,3584]{2,1,0:T(8,128)} %momentum_ref.1, f32[64,3584]{1,0:T(8,128)} %weights_ref.1, s32[1,1,32,56]{3,2,1,0:T(8,128)} %bitcast.1, ...), custom_call_target="tpu_custom_call" | custom-call | tf_op jit(solution)/shard_map/pallas_call | solution.py:378
  13.9 1.2 %shard_map.78 = (f32[1,64,3584]{2,1,0:T(8,128)}, f32[64,3584]{1,0:T(8,128)}) custom-call(f32[64,3584]{1,0:T(8,128)S(1)} %get-tuple-element.6.summed, f32[64,3584]{1,0:T(8,128)S(1)} %get-tuple-element.7.update, f32[64,3584]{1,0:T(8,128)S(1)} %get-tuple-element.8.weights, f32[4,8,128]{2,1,0:T(8,128)S(1)} %get-tuple-element.9.squares), custom_call_target="tpu_custom_call" | custom-call | tf_op jit(solution)/shard_map/pallas_call | solution.py:418
